TPU v7x, 32 devices: a whole 2x2x4 slice. The times are simulated.
32 devices in a mesh: dp: 8 (over z, x), mp: 4 (over y, core).
Axes of the slice: x: 2, y: 2, z: 4, core: 2. Of those that a mesh axis runs over, the one named last changes fastest.
Arguments:
- gating_logits: bfloat16 [8, 3, 64, 7168], P('dp', None, None, 'mp'), may hold values from -6 to 6
- lifted_hidden_values: bfloat16 [8, 3, 64, 7168], P('dp', None, None, 'mp'), may hold values from -6 to 6
- loss_output_grad: bfloat16 [8, 3, 64, 2048], P('dp', None, None, 'mp'), may hold values from -160 to 160
- arrival_flags: int32 [8], P('dp'), may hold values from 0 to 1, as said below
- block_owner_map: int32 [8, 3], P('dp'), may hold values from 0 to 7, as said below
- decoder_multipliers: int32 [8, 3], P('dp'), may hold values from 1 to 4
- block_piece_number: int32 [8], replicated, may hold values from 1 to 2, as said below
Outputs:
- down_grad: float32 [2048, 7168], P('dp', 'mp')
Inputs may be any that keep to these rules, and one draw needn't show every extreme that they name: `arrival_flags`: at least one replica survives. `block_owner_map`: row i lists the partitions (i + r + k) mod 8 for k < 3, with one r for all rows. `block_piece_number`: some partition has exactly 2 live tiles.
All inputs are finite; a program needn't handle non-finite values.
Results may differ from a plain program's by a relative error of at most 0.0042.
Values may be sent and summed in bfloat16 or wider, within the bound.
No kernel may reach another device: no remote copies, remote signals or barrier semaphores. Data moves between devices by JAX's collectives and lax.ppermute only.
A program may use at most 128 MiB of HBM per device.

v0:
```python
import jax
import jax.numpy as jnp
from jax import lax
from jax.sharding import PartitionSpec as P

TILE = 32
CHUNKS = 2


def project(cots, hs):
    return lax.dot_general(cots, hs, (((0,), (0,)), ((), ())), preferred_element_type=jnp.float32)


def on_device(gate, up, cot, flags, owner, mult, pieces):
    _, slots, tok, cols = gate.shape
    feats = cot.shape[3]
    dp = lax.axis_size("dp")
    mp = lax.axis_size("mp")
    outer, inner = (mp, dp // mp)
    i = lax.axis_index("dp")
    z = i // inner
    x = i % inner
    ids = jnp.arange(pieces.shape[0], dtype=jnp.int32)
    tiles = jnp.sum(jnp.where(owner[0][:, None] == ids[None, :], pieces[None, :], 0), axis=1)
    live = tiles * TILE
    weight = flags[0].astype(jnp.float32) * mult[0].astype(jnp.float32)
    tokens = jnp.sum(weight * live.astype(jnp.float32))
    rows = slots * tok
    block = feats // inner
    scaled = (
        (cot[0].astype(jnp.float32) * weight[:, None, None])
        .astype(jnp.bfloat16)
        .reshape(rows, feats)
    )
    if inner == 2:
        swapped = jnp.concatenate([scaled[:, block:], scaled[:, :block]], axis=1)
        scaled = jnp.where(x == 0, scaled, swapped)
    both = ("dp", "mp")
    perm = []
    for a in range(outer):
        for b in range(inner):
            for m in range(mp):
                perm.append(((a * inner + b) * mp + m, (m * inner + b) * mp + (a ^ m)))
    moved = lax.ppermute(scaled, both, perm)
    cots = lax.all_gather(moved, "mp", axis=0, tiled=True)
    total = lax.psum(tokens, "dp")

    def perm_z(pairs):
        return [(a * inner + b, c * inner + b) for a, c in pairs for b in range(inner)]

    sizes = [cols // CHUNKS] * CHUNKS
    lo = 0
    mask = jnp.arange(tok, dtype=jnp.int32)[None, :] < live[:, None]
    outs = []
    for c, w in enumerate(sizes):
        g = gate[0, :, :, lo : lo + w].astype(jnp.float32)
        u = up[0, :, :, lo : lo + w].astype(jnp.float32)
        lo += w
        h = (
            (jax.nn.silu(g) * u * mask[:, :, None].astype(jnp.float32))
            .astype(jnp.bfloat16)
            .reshape(rows, w)
        )
        ha = lax.ppermute(h, "dp", perm_z([(0, 1), (1, 0), (2, 3), (3, 2)]))
        hq = lax.ppermute(h, "dp", perm_z([(0, 2), (2, 0), (1, 3), (3, 1)]))
        hf1 = lax.ppermute(h, "dp", perm_z([(1, 2), (2, 1)]))
        hf2 = lax.ppermute(hq, "dp", perm_z([(1, 0), (2, 3)]))
        hf = jnp.where((z == 1) | (z == 2), hf1, hf2)
        hs = jnp.concatenate([h, ha, hq, hf], axis=0)
        if inner == 2:
            send = project(cots[:, block:], hs).astype(jnp.bfloat16)
            got = lax.ppermute(send, "dp", [(d, d ^ 1) for d in range(dp)])
            outs.append((project(cots[:, :block], hs) + got.astype(jnp.float32)) / total)
        else:
            partial = project(cots, hs).astype(jnp.bfloat16).reshape(inner, block, w)
            groups = [[a * inner + b for b in range(inner)] for a in range(outer)]
            got = lax.all_to_all(partial, "dp", 0, 0, axis_index_groups=groups, tiled=True)
            outs.append(jnp.sum(got.astype(jnp.float32), axis=0) / total)
    return jnp.concatenate(outs, axis=1)


def solution(mesh):
    return jax.shard_map(
        on_device,
        mesh=mesh,
        in_specs=(
            P("dp", None, None, "mp"),
            P("dp", None, None, "mp"),
            P("dp", None, None, "mp"),
            P("dp"),
            P("dp", None),
            P("dp", None),
            P(),
        ),
        out_specs=P("dp", "mp"),
        check_vma=False,
    )
```

profile of v0, /device:TPU:4, one launch (start us, length us, event | category | flops | bytes accessed | tf_op | source)
XLA Modules:
  0.0 109.4 jit_solution(2149252115974620749)
XLA Ops:
  0.0 0.9 select_reduce_fusion
  1.0 1.4 %fusion.24 = (bf16[1,3,64,896]{3,2,1,0:T(8,128)(2,1)S(1)}, bf16[1,3,64,896]{3,2,1,0:T(8,128)(2,1)S(1)}, bf16[1,3,64,896]{3,2,1,0:T(8,128)(2,1)S(1)}, bf16[1,3,64,896]{3,2,1,0:T(8,128)(2,1)S(1)}) fusion(bf16[1,3,64,1792]{3,2,1,0:T(8,128)(2,1)} %param.7, bf16[1,3,64,1792]{3,2,1,0:T(8,128)(2,1)} %param.8), kind=kLoop, calls=%fused_computation.45 | loop fusion | bytes 2752512 | tf_op jit(solution)/shard_map/slice | solution.py:56
  3.1 2.7 %collective-permute-start.2 = (bf16[192,896]{1,0:T(8,128)(2,1)S(1)}, bf16[192,896]{1,0:T(8,128)(2,1)S(1)}, u32[]{:S(2)}, u32[]{:S(2)}) collective-permute-start(bf16[192,896]{1,0:T(8,128)(2,1)S(1)} %get-tuple-element.13), channel_id=1, source_target_pairs={{0,16},{4,20},{16,0},{20,4},{8,24},{12,28},{24,8},{28,12},{1,17},{... | collective-permute-start | bytes 1032200 | tf_op jit(solution)/shard_map/ppermute | solution.py:65
  7.4 2.2 %collective-permute-start = (bf16[192,512]{1,0:T(8,128)(2,1)S(1)}, bf16[192,512]{1,0:T(8,128)(2,1)S(1)}, u32[]{:S(2)}, u32[]{:S(2)}) collective-permute-start(bf16[192,512]{1,0:T(8,128)(2,1)S(1)} %maximum_select_fusion), channel_id=1, source_target_pairs={{0,0},{1,9},{2,18},{3,27},{4,4},{5,13},{6,22},{7,31},{8,1},{9,8},{... | collective-permute-start | bytes 589832 | tf_op jit(solution)/shard_map/ppermute | solution.py:44
  9.6 0.7 collective-permute-start.3
  10.3 4.0 %collective-permute-start.7 = (bf16[192,896]{1,0:T(8,128)(2,1)S(1)}, bf16[192,896]{1,0:T(8,128)(2,1)}, u32[]{:S(2)}, u32[]{:S(2)}) collective-permute-start(bf16[192,896]{1,0:T(8,128)(2,1)S(1)} %get-tuple-element.14), channel_id=1, source_target_pairs={{0,16},{4,20},{16,0},{20,4},{8,24},{12,28},{24,8},{28,12},{1,17},{... | collective-permute-start | bytes 1032200 | tf_op jit(solution)/shard_map/ppermute | solution.py:65
  14.3 15.4 %collective-permute-done.2 = bf16[192,896]{1,0:T(8,128)(2,1)S(1)} collective-permute-done((bf16[192,896]{1,0:T(8,128)(2,1)S(1)}, bf16[192,896]{1,0:T(8,128)(2,1)S(1)}, u32[]{:S(2)}, u32[]{:S(2)}) %collective-permute-start.2) | collective-permute-done | bytes 344096 | tf_op jit(solution)/shard_map/ppermute | solution.py:65
  29.7 1.3 %collective-permute-start.4 = (bf16[192,896]{1,0:T(8,128)(2,1)S(1)}, bf16[192,896]{1,0:T(8,128)(2,1)S(1)}, u32[]{:S(2)}, u32[]{:S(2)}) collective-permute-start(bf16[192,896]{1,0:T(8,128)(2,1)S(1)} %collective-permute-done.2), channel_id=1, source_target_pairs={{8,0},{12,4},{16,24},{20,28},{9,1},{13,5},{17,25},{21,29},{10,2},{... | collective-permute-start | bytes 1032200 | tf_op jit(solution)/shard_map/ppermute | solution.py:67
  31.0 4.0 %collective-permute-start.1 = (bf16[192,896]{1,0:T(8,128)(2,1)S(1)}, bf16[192,896]{1,0:T(8,128)(2,1)}, u32[]{:S(2)}, u32[]{:S(2)}) collective-permute-start(bf16[192,896]{1,0:T(8,128)(2,1)S(1)} %get-tuple-element.13), channel_id=1, source_target_pairs={{0,8},{4,12},{8,0},{12,4},{16,24},{20,28},{24,16},{28,20},{1,9},{5... | collective-permute-start | bytes 1032200 | tf_op jit(solution)/shard_map/ppermute | solution.py:64
  34.9 2.8 %collective-permute-done = bf16[192,512]{1,0:T(8,128)(2,1)S(1)} collective-permute-done((bf16[192,512]{1,0:T(8,128)(2,1)S(1)}, bf16[192,512]{1,0:T(8,128)(2,1)S(1)}, u32[]{:S(2)}, u32[]{:S(2)}) %collective-permute-start) | collective-permute-done | bytes 196640 | tf_op jit(solution)/shard_map/ppermute | solution.py:44
  37.8 0.7 collective-permute-start.8
  38.4 7.5 %all_gather.3 = bf16[768,512]{1,0:T(8,128)(2,1)S(1)} all-gather(bf16[192,512]{1,0:T(8,128)(2,1)S(1)} %collective-permute-done), channel_id=1, replica_groups=mesh['dp'=8,'mp'=4] {'mp'}, dimensions={0}, use_global_device_ids=true | all-gather | bytes 983040 | tf_op jit(solution)/shard_map/all_gather | solution.py:45
  45.9 4.2 %collective-permute-start.6 = (bf16[192,896]{1,0:T(8,128)(2,1)S(1)}, bf16[192,896]{1,0:T(8,128)(2,1)S(1)}, u32[]{:S(2)}, u32[]{:S(2)}) collective-permute-start(bf16[192,896]{1,0:T(8,128)(2,1)S(1)} %get-tuple-element.14), channel_id=1, source_target_pairs={{0,8},{4,12},{8,0},{12,4},{16,24},{20,28},{24,16},{28,20},{1,9},{5... | collective-permute-start | bytes 1032200 | tf_op jit(solution)/shard_map/ppermute | solution.py:64
  50.1 1.3 %collective-permute-start.9 = (bf16[192,896]{1,0:T(8,128)(2,1)}, bf16[192,896]{1,0:T(8,128)(2,1)S(1)}, u32[]{:S(2)}, u32[]{:S(2)}) collective-permute-start(bf16[192,896]{1,0:T(8,128)(2,1)} %collective-permute-done.7), channel_id=1, source_target_pairs={{8,0},{12,4},{16,24},{20,28},{9,1},{13,5},{17,25},{21,29},{10,2},{... | collective-permute-start | bytes 1032200 | tf_op jit(solution)/shard_map/ppermute | solution.py:67
  51.4 6.4 %collective-permute-done.1 = bf16[192,896]{1,0:T(8,128)(2,1)} collective-permute-done((bf16[192,896]{1,0:T(8,128)(2,1)S(1)}, bf16[192,896]{1,0:T(8,128)(2,1)}, u32[]{:S(2)}, u32[]{:S(2)}) %collective-permute-start.1) | collective-permute-done | bytes 344096 | tf_op jit(solution)/shard_map/ppermute | solution.py:64
  57.8 1.6 %convolution_convert_fusion.1 = bf16[256,896]{1,0:T(8,128)(2,1)S(1)} fusion(bf16[768,512]{1,0:T(8,128)(2,1)S(1)} %all_gather.3, bf16[192,896]{1,0:T(8,128)(2,1)S(1)} %broadcast_select_fusion.1, bf16[192,896]{1,0:T(8,128)(2,1)S(1)} %collective-permute-done.2, bf16[192,896]{1,0:T(8,128)(2,1)} %collective-permute-done.1, bf16[192,896]{1,0:T(8,128)(2,1)S(1)} %get-tuple-element.13), kind=kOutput, calls=%fused_computation.8 | convolution fusion | flops 358055936 | bytes 2228224 | tf_op jit(solution)/shard_map/dot_general | solution.py:11
  59.4 1.6 %collective-permute-start.5 = (bf16[256,896]{1,0:T(8,128)(2,1)S(1)}, bf16[256,896]{1,0:T(8,128)(2,1)S(1)}, u32[]{:S(2)}, u32[]{:S(2)}) collective-permute-start(bf16[256,896]{1,0:T(8,128)(2,1)S(1)} %convolution_convert_fusion.1), channel_id=1, source_target_pairs={{0,4},{4,0},{8,12},{12,8},{16,20},{20,16},{24,28},{28,24},{1,5},{5... | collective-permute-start | bytes 1376264 | tf_op jit(solution)/shard_map/ppermute | solution.py:72
  61.0 11.1 %collective-permute-done.9 = bf16[192,896]{1,0:T(8,128)(2,1)S(1)} collective-permute-done((bf16[192,896]{1,0:T(8,128)(2,1)}, bf16[192,896]{1,0:T(8,128)(2,1)S(1)}, u32[]{:S(2)}, u32[]{:S(2)}) %collective-permute-start.9) | collective-permute-done | bytes 344096 | tf_op jit(solution)/shard_map/ppermute | solution.py:67
  72.2 2.5 %convolution_convert_fusion = bf16[256,896]{1,0:T(8,128)(2,1)} fusion(bf16[768,512]{1,0:T(8,128)(2,1)S(1)} %all_gather.3, bf16[192,896]{1,0:T(8,128)(2,1)S(1)} %broadcast_select_fusion, bf16[192,896]{1,0:T(8,128)(2,1)} %collective-permute-done.7, bf16[192,896]{1,0:T(8,128)(2,1)S(1)} %collective-permute-done.6, bf16[192,896]{1,0:T(8,128)(2,1)S(1)} %get-tuple-element.14), kind=kOutput, calls=%fused_computation.7 | convolution fusion | flops 358055936 | bytes 2228224 | tf_op jit(solution)/shard_map/dot_general | solution.py:11
  74.7 1.5 %collective-permute-start.10 = (bf16[256,896]{1,0:T(8,128)(2,1)}, bf16[256,896]{1,0:T(8,128)(2,1)}, u32[]{:S(2)}, u32[]{:S(2)}) collective-permute-start(bf16[256,896]{1,0:T(8,128)(2,1)} %convolution_convert_fusion), channel_id=1, source_target_pairs={{0,4},{4,0},{8,12},{12,8},{16,20},{20,16},{24,28},{28,24},{1,5},{5... | collective-permute-start | bytes 1376264 | tf_op jit(solution)/shard_map/ppermute | solution.py:72
  76.2 27.1 %psum.7 = f32[]{:T(128)} all-reduce(f32[]{:T(128)} %get-tuple-element.5), channel_id=1, replica_groups=mesh['dp'=8,'mp'=4] {'dp'}, use_global_device_ids=true, to_apply=%region_2.3 | all-reduce | flops 1 | bytes 8 | tf_op jit(solution)/shard_map/psum | solution.py:46
  103.3 2.3 %fusion.1 = f32[256,896]{1,0:T(8,128)S(1)} fusion(bf16[256,896]{1,0:T(8,128)(2,1)S(1)} %collective-permute-done.5, f32[]{:T(128)} %psum.7, bf16[768,512]{1,0:T(8,128)(2,1)S(1)} %all_gather.3, bf16[192,896]{1,0:T(8,128)(2,1)S(1)} %broadcast_select_fusion.1, bf16[192,896]{1,0:T(8,128)(2,1)S(1)} %copy-done.3, bf16[192,896]{1,0:T(8,128)(2,1)} %collective-permute-done.1, ...), kind=kOutput, calls=%fused_computation.6 | convolution fusion | flops 358514688 | bytes 3145732 | tf_op jit(solution)/shard_map/dot_general | solution.py:11
  105.6 2.4 %fusion = f32[256,896]{1,0:T(8,128)S(1)} fusion(bf16[256,896]{1,0:T(8,128)(2,1)} %collective-permute-done.10, f32[]{:T(128)} %psum.7, bf16[768,512]{1,0:T(8,128)(2,1)S(1)} %all_gather.3, bf16[192,896]{1,0:T(8,128)(2,1)S(1)} %broadcast_select_fusion, bf16[192,896]{1,0:T(8,128)(2,1)} %collective-permute-done.7, bf16[192,896]{1,0:T(8,128)(2,1)S(1)} %copy-done.5, ...), kind=kOutput, calls=%fused_computation.4 | convolution fusion | flops 358514688 | bytes 3145732 | tf_op jit(solution)/shard_map/dot_general | solution.py:11
  108.0 1.4 %pad_maximum_fusion = f32[256,1792]{1,0:T(8,128)} fusion(f32[256,896]{1,0:T(8,128)S(1)} %fusion, f32[256,896]{1,0:T(8,128)S(1)} %fusion.1), kind=kLoop, calls=%fused_computation | loop fusion | flops 458752 | bytes 3670016 | tf_op jit(solution)/shard_map/concatenate | solution.py:79
  (31 shorter events, 1.8 us)
Async XLA Ops:
  1.0 5.4 %copy-start.1 = (s32[1,3]{1,0:T(1,128)S(1)}, s32[1,3]{1,0:T(1,128)}, u32[]{:S(2)}) copy-start(s32[1,3]{1,0:T(1,128)} %param.12) | copy-start | bytes 40
  1.0 6.1 %copy-start = (bf16[1,3,64,512]{3,2,1,0:T(8,128)(2,1)S(1)}, bf16[1,3,64,512]{3,2,1,0:T(8,128)(2,1)}, u32[]{:S(2)}) copy-start(bf16[1,3,64,512]{3,2,1,0:T(8,128)(2,1)} %param.9) | copy-start | bytes 589828
  3.1 26.6 %collective-permute-start.2 = (bf16[192,896]{1,0:T(8,128)(2,1)S(1)}, bf16[192,896]{1,0:T(8,128)(2,1)S(1)}, u32[]{:S(2)}, u32[]{:S(2)}) collective-permute-start(bf16[192,896]{1,0:T(8,128)(2,1)S(1)} %get-tuple-element.13), channel_id=1, source_target_pairs={{0,16},{4,20},{16,0},{20,4},{8,24},{12,28},{24,8},{28,12},{1,17},{... | collective-permute-start | bytes 1032200 | tf_op jit(solution)/shard_map/ppermute | solution.py:65
  7.4 30.4 %collective-permute-start = (bf16[192,512]{1,0:T(8,128)(2,1)S(1)}, bf16[192,512]{1,0:T(8,128)(2,1)S(1)}, u32[]{:S(2)}, u32[]{:S(2)}) collective-permute-start(bf16[192,512]{1,0:T(8,128)(2,1)S(1)} %maximum_select_fusion), channel_id=1, source_target_pairs={{0,0},{1,9},{2,18},{3,27},{4,4},{5,13},{6,22},{7,31},{8,1},{9,8},{... | collective-permute-start | bytes 589832 | tf_op jit(solution)/shard_map/ppermute | solution.py:44
  9.6 36.3 %collective-permute-start.3 = (bf16[192,896]{1,0:T(8,128)(2,1)S(1)}, bf16[192,896]{1,0:T(8,128)(2,1)S(1)}, u32[]{:S(2)}, u32[]{:S(2)}) collective-permute-start(bf16[192,896]{1,0:T(8,128)(2,1)S(1)} %get-tuple-element.13), channel_id=1, source_target_pairs={{8,16},{12,20},{16,8},{20,12},{9,17},{13,21},{17,9},{21,13},{10,18... | collective-permute-start | bytes 1032200 | tf_op jit(solution)/shard_map/ppermute | solution.py:66
  10.3 39.7 %collective-permute-start.7 = (bf16[192,896]{1,0:T(8,128)(2,1)S(1)}, bf16[192,896]{1,0:T(8,128)(2,1)}, u32[]{:S(2)}, u32[]{:S(2)}) collective-permute-start(bf16[192,896]{1,0:T(8,128)(2,1)S(1)} %get-tuple-element.14), channel_id=1, source_target_pairs={{0,16},{4,20},{16,0},{20,4},{8,24},{12,28},{24,8},{28,12},{1,17},{... | collective-permute-start | bytes 1032200 | tf_op jit(solution)/shard_map/ppermute | solution.py:65
  29.7 28.1 %copy-start.2 = (bf16[192,896]{1,0:T(8,128)(2,1)}, bf16[192,896]{1,0:T(8,128)(2,1)S(1)}, u32[]{:S(2)}) copy-start(bf16[192,896]{1,0:T(8,128)(2,1)S(1)} %collective-permute-done.2) | copy-start | bytes 1032196
  29.7 21.7 %collective-permute-start.4 = (bf16[192,896]{1,0:T(8,128)(2,1)S(1)}, bf16[192,896]{1,0:T(8,128)(2,1)S(1)}, u32[]{:S(2)}, u32[]{:S(2)}) collective-permute-start(bf16[192,896]{1,0:T(8,128)(2,1)S(1)} %collective-permute-done.2), channel_id=1, source_target_pairs={{8,0},{12,4},{16,24},{20,28},{9,1},{13,5},{17,25},{21,29},{10,2},{... | collective-permute-start | bytes 1032200 | tf_op jit(solution)/shard_map/ppermute | solution.py:67
  31.0 26.8 %collective-permute-start.1 = (bf16[192,896]{1,0:T(8,128)(2,1)S(1)}, bf16[192,896]{1,0:T(8,128)(2,1)}, u32[]{:S(2)}, u32[]{:S(2)}) collective-permute-start(bf16[192,896]{1,0:T(8,128)(2,1)S(1)} %get-tuple-element.13), channel_id=1, source_target_pairs={{0,8},{4,12},{8,0},{12,4},{16,24},{20,28},{24,16},{28,20},{1,9},{5... | collective-permute-start | bytes 1032200 | tf_op jit(solution)/shard_map/ppermute | solution.py:64
  37.8 23.2 %collective-permute-start.8 = (bf16[192,896]{1,0:T(8,128)(2,1)S(1)}, bf16[192,896]{1,0:T(8,128)(2,1)S(1)}, u32[]{:S(2)}, u32[]{:S(2)}) collective-permute-start(bf16[192,896]{1,0:T(8,128)(2,1)S(1)} %get-tuple-element.14), channel_id=1, source_target_pairs={{8,16},{12,20},{16,8},{20,12},{9,17},{13,21},{17,9},{21,13},{10,18... | collective-permute-start | bytes 1032200 | tf_op jit(solution)/shard_map/ppermute | solution.py:66
  45.9 26.2 %collective-permute-start.6 = (bf16[192,896]{1,0:T(8,128)(2,1)S(1)}, bf16[192,896]{1,0:T(8,128)(2,1)S(1)}, u32[]{:S(2)}, u32[]{:S(2)}) collective-permute-start(bf16[192,896]{1,0:T(8,128)(2,1)S(1)} %get-tuple-element.14), channel_id=1, source_target_pairs={{0,8},{4,12},{8,0},{12,4},{16,24},{20,28},{24,16},{28,20},{1,9},{5... | collective-permute-start | bytes 1032200 | tf_op jit(solution)/shard_map/ppermute | solution.py:64
  50.1 22.0 %collective-permute-start.9 = (bf16[192,896]{1,0:T(8,128)(2,1)}, bf16[192,896]{1,0:T(8,128)(2,1)S(1)}, u32[]{:S(2)}, u32[]{:S(2)}) collective-permute-start(bf16[192,896]{1,0:T(8,128)(2,1)} %collective-permute-done.7), channel_id=1, source_target_pairs={{8,0},{12,4},{16,24},{20,28},{9,1},{13,5},{17,25},{21,29},{10,2},{... | collective-permute-start | bytes 1032200 | tf_op jit(solution)/shard_map/ppermute | solution.py:67
  59.4 43.9 %collective-permute-start.5 = (bf16[256,896]{1,0:T(8,128)(2,1)S(1)}, bf16[256,896]{1,0:T(8,128)(2,1)S(1)}, u32[]{:S(2)}, u32[]{:S(2)}) collective-permute-start(bf16[256,896]{1,0:T(8,128)(2,1)S(1)} %convolution_convert_fusion.1), channel_id=1, source_target_pairs={{0,4},{4,0},{8,12},{12,8},{16,20},{20,16},{24,28},{28,24},{1,5},{5... | collective-permute-start | bytes 1376264 | tf_op jit(solution)/shard_map/ppermute | solution.py:72
  72.1 31.1 %copy-start.3 = (bf16[192,896]{1,0:T(8,128)(2,1)S(1)}, bf16[192,896]{1,0:T(8,128)(2,1)}, u32[]{:S(2)}) copy-start(bf16[192,896]{1,0:T(8,128)(2,1)} %copy-done.2) | copy-start | bytes 1032196
  72.2 2.5 %copy-start.4 = (bf16[192,896]{1,0:T(8,128)(2,1)}, bf16[192,896]{1,0:T(8,128)(2,1)S(1)}, u32[]{:S(2)}) copy-start(bf16[192,896]{1,0:T(8,128)(2,1)S(1)} %collective-permute-done.6) | copy-start | bytes 1032196
  74.7 30.9 %collective-permute-start.10 = (bf16[256,896]{1,0:T(8,128)(2,1)}, bf16[256,896]{1,0:T(8,128)(2,1)}, u32[]{:S(2)}, u32[]{:S(2)}) collective-permute-start(bf16[256,896]{1,0:T(8,128)(2,1)} %convolution_convert_fusion), channel_id=1, source_target_pairs={{0,4},{4,0},{8,12},{12,8},{16,20},{20,16},{24,28},{28,24},{1,5},{5... | collective-permute-start | bytes 1376264 | tf_op jit(solution)/shard_map/ppermute | solution.py:72
  103.3 2.3 %copy-start.5 = (bf16[192,896]{1,0:T(8,128)(2,1)S(1)}, bf16[192,896]{1,0:T(8,128)(2,1)}, u32[]{:S(2)}) copy-start(bf16[192,896]{1,0:T(8,128)(2,1)} %copy-done.4) | copy-start | bytes 1032196
where the time goes:
time: 110 us; the launch traced here: 109 us
  waiting for transfers between devices  35.7 us (32%)
  blocking collectives  34.6 us (31%)
  starting transfers between devices  24 us (22%)
  matrix products  8.79 us (8%)
  other arithmetic  3.76 us (3%)
  local copies, waits for them, and re-layouts  1.72 us (2%)
    psum x1, blocking collectives, on_device(): total = lax.psum(tokens, 'dp')  27.1 us
    ppermute x2, waiting for transfers between devices, on_device(): hq = lax.ppermute(h, 'dp', perm_z([(0, 2), (2, 0), (1, 3), (3, 1)]))  15.4 us
    ppermute x2, waiting for transfers between devices, on_device(): hf2 = lax.ppermute(hq, 'dp', perm_z([(1, 0), (2, 3)]))  11.1 us
    dot_general x4, matrix products, project(): lax.dot_general(cots, hs, (((0,), (0,)), ((), ())), preferred_element_typ...  8.79 us
    ppermute x2, starting transfers between devices, on_device(): ha = lax.ppermute(h, 'dp', perm_z([(0, 1), (1, 0), (2, 3), (3, 2)]))  8.11 us
    all_gather x1, blocking collectives, on_device(): cots = lax.all_gather(moved, 'mp', axis=0, tiled=True)  7.47 us
    ppermute x2, starting transfers between devices, on_device(): hq = lax.ppermute(h, 'dp', perm_z([(0, 2), (2, 0), (1, 3), (3, 1)]))  6.66 us
    ppermute x2, waiting for transfers between devices, on_device(): ha = lax.ppermute(h, 'dp', perm_z([(0, 1), (1, 0), (2, 3), (3, 2)]))  6.41 us
  transfers between devices with their start and end apart: 11, of which 4 were waited for; matrix products, arithmetic and copies ran while one was open for 7% of the time, Pallas kernels for 0%

commit v1 on v0

--- a/solution.py
+++ b/solution.py
@@ -2,6 +2,7 @@
 import jax.numpy as jnp
 from jax import lax
 from jax.sharding import PartitionSpec as P
+from jax.lax import all_to_all, axis_size
 
 TILE = 32
 CHUNKS = 2
@@ -42,7 +43,9 @@
             for m in range(mp):
                 perm.append(((a * inner + b) * mp + m, (m * inner + b) * mp + (a ^ m)))
     moved = lax.ppermute(scaled, both, perm)
-    cots = lax.all_gather(moved, "mp", axis=0, tiled=True)
+    cots = jnp.concatenate(
+        all_to_all(jnp.stack([moved for _ in range(axis_size("mp"))]), "mp", 0, 0), axis=0
+    )
     total = lax.psum(tokens, "dp")
 
     def perm_z(pairs):

time: 110 us -> 109 us (level)
  blocking collectives: 34.6 us -> 27.1 us
  waiting for transfers between devices: 35.7 us -> 40.9 us
    all_gather x1 -> x0, blocking collectives: 7.47 us -> none  [on_device(): cots = lax.all_gather(moved, 'mp', axis=0, tiled=True)]
    ppermute x1, waiting for transfers between devices: 2.82 us -> 6.77 us  [on_device(): moved = lax.ppermute(scaled, both, perm)]
    all_to_all x0 -> x1, starting transfers between devices: none -> 3.48 us  [on_device(): all_to_all(jnp.stack([moved for _ in range(axis_size('mp'))]), 'mp', 0, 0)]
    ppermute x2, starting transfers between devices: 8.11 us -> 5.13 us  [on_device(): ha = lax.ppermute(h, 'dp', perm_z([(0, 1), (1, 0), (2, 3), (3, 2)]))]
  transfers between devices with their start and end apart: 11 -> 12, of which waited for: 4 -> 5; matrix products, arithmetic and copies ran while one was open for 7% -> 8% of each run, Pallas kernels for 0% -> 0%
where the time goes in v1:
time: 109 us; the launch traced here: 108 us
  waiting for transfers between devices  40.9 us (38%)
  blocking collectives  27.1 us (25%)
  starting transfers between devices  24.5 us (22%)
  matrix products  8.62 us (8%)
  other arithmetic  3.84 us (4%)
  local copies, waits for them, and re-layouts  2.65 us (2%)
    psum x1, blocking collectives, on_device(): total = lax.psum(tokens, 'dp')  27.1 us
    ppermute x2, waiting for transfers between devices, on_device(): hq = lax.ppermute(h, 'dp', perm_z([(0, 2), (2, 0), (1, 3), (3, 1)]))  15.3 us
    ppermute x2, waiting for transfers between devices, on_device(): hf2 = lax.ppermute(hq, 'dp', perm_z([(1, 0), (2, 3)]))  11.4 us
    dot_general x4, matrix products, project(): lax.dot_general(cots, hs, (((0,), (0,)), ((), ())), preferred_element_typ...  8.62 us
    ppermute x2, waiting for transfers between devices, on_device(): ha = lax.ppermute(h, 'dp', perm_z([(0, 1), (1, 0), (2, 3), (3, 2)]))  7.44 us
    ppermute x1, waiting for transfers between devices, on_device(): moved = lax.ppermute(scaled, both, perm)  6.77 us
    ppermute x2, starting transfers between devices, on_device(): hq = lax.ppermute(h, 'dp', perm_z([(0, 2), (2, 0), (1, 3), (3, 1)]))  6.66 us
    ppermute x2, starting transfers between devices, on_device(): ha = lax.ppermute(h, 'dp', perm_z([(0, 1), (1, 0), (2, 3), (3, 2)]))  5.13 us
  transfers between devices with their start and end apart: 12, of which 5 were waited for; matrix products, arithmetic and copies ran while one was open for 8% of the time, Pallas kernels for 0%

profile of v1, /device:TPU:4, one launch (start us, length us, event | category | flops | bytes accessed | tf_op | source)
XLA Modules:
  0.0 108.4 jit_solution(750028796801393868)
XLA Ops:
  0.0 0.9 select_reduce_fusion
  1.0 1.4 %fusion.24 = (bf16[1,3,64,896]{3,2,1,0:T(8,128)(2,1)S(1)}, bf16[1,3,64,896]{3,2,1,0:T(8,128)(2,1)S(1)}, bf16[1,3,64,896]{3,2,1,0:T(8,128)(2,1)S(1)}, bf16[1,3,64,896]{3,2,1,0:T(8,128)(2,1)S(1)}) fusion(bf16[1,3,64,1792]{3,2,1,0:T(8,128)(2,1)} %param.7, bf16[1,3,64,1792]{3,2,1,0:T(8,128)(2,1)} %param.8), kind=kLoop, calls=%fused_computation.45 | loop fusion | bytes 2752512 | tf_op jit(solution)/shard_map/slice | solution.py:59
  3.1 2.7 %collective-permute-start.2 = (bf16[192,896]{1,0:T(8,128)(2,1)S(1)}, bf16[192,896]{1,0:T(8,128)(2,1)S(1)}, u32[]{:S(2)}, u32[]{:S(2)}) collective-permute-start(bf16[192,896]{1,0:T(8,128)(2,1)S(1)} %get-tuple-element.13), channel_id=1, source_target_pairs={{0,16},{4,20},{16,0},{20,4},{8,24},{12,28},{24,8},{28,12},{1,17},{... | collective-permute-start | bytes 1032200 | tf_op jit(solution)/shard_map/ppermute | solution.py:68
  7.5 2.2 %collective-permute-start = (bf16[192,512]{1,0:T(8,128)(2,1)S(1)}, bf16[192,512]{1,0:T(8,128)(2,1)S(1)}, u32[]{:S(2)}, u32[]{:S(2)}) collective-permute-start(bf16[192,512]{1,0:T(8,128)(2,1)S(1)} %maximum_select_fusion), channel_id=1, source_target_pairs={{0,0},{1,9},{2,18},{3,27},{4,4},{5,13},{6,22},{7,31},{8,1},{9,8},{... | collective-permute-start | bytes 589832 | tf_op jit(solution)/shard_map/ppermute | solution.py:45
  9.7 0.7 collective-permute-start.3
  10.4 4.0 %collective-permute-start.7 = (bf16[192,896]{1,0:T(8,128)(2,1)S(1)}, bf16[192,896]{1,0:T(8,128)(2,1)}, u32[]{:S(2)}, u32[]{:S(2)}) collective-permute-start(bf16[192,896]{1,0:T(8,128)(2,1)S(1)} %get-tuple-element.14), channel_id=1, source_target_pairs={{0,16},{4,20},{16,0},{20,4},{8,24},{12,28},{24,8},{28,12},{1,17},{... | collective-permute-start | bytes 1032200 | tf_op jit(solution)/shard_map/ppermute | solution.py:68
  14.4 15.3 %collective-permute-done.2 = bf16[192,896]{1,0:T(8,128)(2,1)S(1)} collective-permute-done((bf16[192,896]{1,0:T(8,128)(2,1)S(1)}, bf16[192,896]{1,0:T(8,128)(2,1)S(1)}, u32[]{:S(2)}, u32[]{:S(2)}) %collective-permute-start.2) | collective-permute-done | bytes 344096 | tf_op jit(solution)/shard_map/ppermute | solution.py:68
  29.7 1.3 %collective-permute-start.4 = (bf16[192,896]{1,0:T(8,128)(2,1)S(1)}, bf16[192,896]{1,0:T(8,128)(2,1)S(1)}, u32[]{:S(2)}, u32[]{:S(2)}) collective-permute-start(bf16[192,896]{1,0:T(8,128)(2,1)S(1)} %collective-permute-done.2), channel_id=1, source_target_pairs={{8,0},{12,4},{16,24},{20,28},{9,1},{13,5},{17,25},{21,29},{10,2},{... | collective-permute-start | bytes 1032200 | tf_op jit(solution)/shard_map/ppermute | solution.py:70
  31.0 6.8 %collective-permute-done = bf16[192,512]{1,0:T(8,128)(2,1)S(1)} collective-permute-done((bf16[192,512]{1,0:T(8,128)(2,1)S(1)}, bf16[192,512]{1,0:T(8,128)(2,1)S(1)}, u32[]{:S(2)}, u32[]{:S(2)}) %collective-permute-start) | collective-permute-done | bytes 196640 | tf_op jit(solution)/shard_map/ppermute | solution.py:45
  37.8 0.9 stack.2
  38.7 3.5 %all-to-all-start = ((bf16[4,192,512]{2,1,0:T(8,128)(2,1)}), bf16[4,192,512]{2,1,0:T(8,128)(2,1)S(1)}, u32[]{:S(2)}, u32[]{:S(2)}) async-start(bf16[4,192,512]{2,1,0:T(8,128)(2,1)} %stack.2), calls=%async_computation | async-start | bytes 1572864 | tf_op jit(solution)/shard_map/all_to_all | solution.py:47
  43.2 4.8 %collective-permute-start.6 = (bf16[192,896]{1,0:T(8,128)(2,1)S(1)}, bf16[192,896]{1,0:T(8,128)(2,1)}, u32[]{:S(2)}, u32[]{:S(2)}) collective-permute-start(bf16[192,896]{1,0:T(8,128)(2,1)S(1)} %get-tuple-element.14), channel_id=1, source_target_pairs={{0,8},{4,12},{8,0},{12,4},{16,24},{20,28},{24,16},{28,20},{1,9},{5... | collective-permute-start | bytes 1032200 | tf_op jit(solution)/shard_map/ppermute | solution.py:67
  48.0 1.3 %collective-permute-start.9 = (bf16[192,896]{1,0:T(8,128)(2,1)}, bf16[192,896]{1,0:T(8,128)(2,1)S(1)}, u32[]{:S(2)}, u32[]{:S(2)}) collective-permute-start(bf16[192,896]{1,0:T(8,128)(2,1)} %collective-permute-done.7), channel_id=1, source_target_pairs={{8,0},{12,4},{16,24},{20,28},{9,1},{13,5},{17,25},{21,29},{10,2},{... | collective-permute-start | bytes 1032200 | tf_op jit(solution)/shard_map/ppermute | solution.py:70
  49.3 1.0 collective-permute-done.4
  50.4 7.4 %collective-permute-done.1 = bf16[192,896]{1,0:T(8,128)(2,1)} collective-permute-done((bf16[192,896]{1,0:T(8,128)(2,1)S(1)}, bf16[192,896]{1,0:T(8,128)(2,1)}, u32[]{:S(2)}, u32[]{:S(2)}) %collective-permute-start.1) | collective-permute-done | bytes 344096 | tf_op jit(solution)/shard_map/ppermute | solution.py:67
  57.8 2.3 %convolution_convert_fusion.1 = bf16[256,896]{1,0:T(8,128)(2,1)} fusion(bf16[768,512]{1,0:T(8,128)(2,1)S(1)} %bitcast.23, bf16[192,896]{1,0:T(8,128)(2,1)S(1)} %broadcast_select_fusion.1, bf16[192,896]{1,0:T(8,128)(2,1)S(1)} %collective-permute-done.2, bf16[192,896]{1,0:T(8,128)(2,1)} %collective-permute-done.1, bf16[192,896]{1,0:T(8,128)(2,1)S(1)} %get-tuple-element.13), kind=kOutput, calls=%fused_computation.8 | convolution fusion | flops 358055936 | bytes 2228224 | tf_op jit(solution)/shard_map/dot_general | solution.py:12
  60.2 1.5 %collective-permute-start.5 = (bf16[256,896]{1,0:T(8,128)(2,1)}, bf16[256,896]{1,0:T(8,128)(2,1)}, u32[]{:S(2)}, u32[]{:S(2)}) collective-permute-start(bf16[256,896]{1,0:T(8,128)(2,1)} %convolution_convert_fusion.1), channel_id=1, source_target_pairs={{0,4},{4,0},{8,12},{12,8},{16,20},{20,16},{24,28},{28,24},{1,5},{5... | collective-permute-start | bytes 1376264 | tf_op jit(solution)/shard_map/ppermute | solution.py:75
  61.7 10.4 %collective-permute-done.9 = bf16[192,896]{1,0:T(8,128)(2,1)S(1)} collective-permute-done((bf16[192,896]{1,0:T(8,128)(2,1)}, bf16[192,896]{1,0:T(8,128)(2,1)S(1)}, u32[]{:S(2)}, u32[]{:S(2)}) %collective-permute-start.9) | collective-permute-done | bytes 344096 | tf_op jit(solution)/shard_map/ppermute | solution.py:70
  72.1 1.7 %convolution_convert_fusion = bf16[256,896]{1,0:T(8,128)(2,1)S(1)} fusion(bf16[768,512]{1,0:T(8,128)(2,1)S(1)} %bitcast.24, bf16[192,896]{1,0:T(8,128)(2,1)S(1)} %broadcast_select_fusion, bf16[192,896]{1,0:T(8,128)(2,1)} %collective-permute-done.7, bf16[192,896]{1,0:T(8,128)(2,1)} %collective-permute-done.6, bf16[192,896]{1,0:T(8,128)(2,1)S(1)} %get-tuple-element.14), kind=kOutput, calls=%fused_computation.7 | convolution fusion | flops 358055936 | bytes 2228224 | tf_op jit(solution)/shard_map/dot_general | solution.py:12
  73.8 1.6 %collective-permute-start.10 = (bf16[256,896]{1,0:T(8,128)(2,1)S(1)}, bf16[256,896]{1,0:T(8,128)(2,1)S(1)}, u32[]{:S(2)}, u32[]{:S(2)}) collective-permute-start(bf16[256,896]{1,0:T(8,128)(2,1)S(1)} %convolution_convert_fusion), channel_id=1, source_target_pairs={{0,4},{4,0},{8,12},{12,8},{16,20},{20,16},{24,28},{28,24},{1,5},{5... | collective-permute-start | bytes 1376264 | tf_op jit(solution)/shard_map/ppermute | solution.py:75
  75.4 27.1 %psum.7 = f32[]{:T(128)} all-reduce(f32[]{:T(128)} %get-tuple-element.5), channel_id=1, replica_groups=mesh['dp'=8,'mp'=4] {'dp'}, use_global_device_ids=true, to_apply=%region_2.3 | all-reduce | flops 1 | bytes 8 | tf_op jit(solution)/shard_map/psum | solution.py:49
  102.5 2.4 %fusion.1 = f32[256,896]{1,0:T(8,128)S(1)} fusion(bf16[256,896]{1,0:T(8,128)(2,1)} %collective-permute-done.5, f32[]{:T(128)} %psum.7, bf16[768,512]{1,0:T(8,128)(2,1)S(1)} %bitcast.25, bf16[192,896]{1,0:T(8,128)(2,1)S(1)} %broadcast_select_fusion.1, bf16[192,896]{1,0:T(8,128)(2,1)} %copy-done.2, bf16[192,896]{1,0:T(8,128)(2,1)} %collective-permute-done.1, ...), kind=kOutput, calls=%fused_computation.6 | convolution fusion | flops 358514688 | bytes 3145732 | tf_op jit(solution)/shard_map/dot_general | solution.py:12
  104.9 2.2 %fusion = f32[256,896]{1,0:T(8,128)S(1)} fusion(bf16[256,896]{1,0:T(8,128)(2,1)S(1)} %collective-permute-done.10, f32[]{:T(128)} %psum.7, bf16[768,512]{1,0:T(8,128)(2,1)S(1)} %bitcast.26, bf16[192,896]{1,0:T(8,128)(2,1)S(1)} %broadcast_select_fusion, bf16[192,896]{1,0:T(8,128)(2,1)} %collective-permute-done.7, bf16[192,896]{1,0:T(8,128)(2,1)} %collective-permute-done.6, ...), kind=kOutput, calls=%fused_computation.4 | convolution fusion | flops 358514688 | bytes 3145732 | tf_op jit(solution)/shard_map/dot_general | solution.py:12
  107.1 1.4 %pad_maximum_fusion = f32[256,1792]{1,0:T(8,128)} fusion(f32[256,896]{1,0:T(8,128)S(1)} %fusion, f32[256,896]{1,0:T(8,128)S(1)} %fusion.1), kind=kLoop, calls=%fused_computation | loop fusion | flops 458752 | bytes 3670016 | tf_op jit(solution)/shard_map/concatenate | solution.py:82
  (27 shorter events, 2.9 us)
Async XLA Ops:
  1.0 5.4 %copy-start.1 = (s32[1,3]{1,0:T(1,128)S(1)}, s32[1,3]{1,0:T(1,128)}, u32[]{:S(2)}) copy-start(s32[1,3]{1,0:T(1,128)} %param.12) | copy-start | bytes 40
  1.0 6.2 %copy-start = (bf16[1,3,64,512]{3,2,1,0:T(8,128)(2,1)S(1)}, bf16[1,3,64,512]{3,2,1,0:T(8,128)(2,1)}, u32[]{:S(2)}) copy-start(bf16[1,3,64,512]{3,2,1,0:T(8,128)(2,1)} %param.9) | copy-start | bytes 589828
  3.1 26.6 %collective-permute-start.2 = (bf16[192,896]{1,0:T(8,128)(2,1)S(1)}, bf16[192,896]{1,0:T(8,128)(2,1)S(1)}, u32[]{:S(2)}, u32[]{:S(2)}) collective-permute-start(bf16[192,896]{1,0:T(8,128)(2,1)S(1)} %get-tuple-element.13), channel_id=1, source_target_pairs={{0,16},{4,20},{16,0},{20,4},{8,24},{12,28},{24,8},{28,12},{1,17},{... | collective-permute-start | bytes 1032200 | tf_op jit(solution)/shard_map/ppermute | solution.py:68
  7.5 30.3 %collective-permute-start = (bf16[192,512]{1,0:T(8,128)(2,1)S(1)}, bf16[192,512]{1,0:T(8,128)(2,1)S(1)}, u32[]{:S(2)}, u32[]{:S(2)}) collective-permute-start(bf16[192,512]{1,0:T(8,128)(2,1)S(1)} %maximum_select_fusion), channel_id=1, source_target_pairs={{0,0},{1,9},{2,18},{3,27},{4,4},{5,13},{6,22},{7,31},{8,1},{9,8},{... | collective-permute-start | bytes 589832 | tf_op jit(solution)/shard_map/ppermute | solution.py:45
  9.7 33.4 %collective-permute-start.3 = (bf16[192,896]{1,0:T(8,128)(2,1)S(1)}, bf16[192,896]{1,0:T(8,128)(2,1)S(1)}, u32[]{:S(2)}, u32[]{:S(2)}) collective-permute-start(bf16[192,896]{1,0:T(8,128)(2,1)S(1)} %get-tuple-element.13), channel_id=1, source_target_pairs={{8,16},{12,20},{16,8},{20,12},{9,17},{13,21},{17,9},{21,13},{10,18... | collective-permute-start | bytes 1032200 | tf_op jit(solution)/shard_map/ppermute | solution.py:69
  10.4 37.6 %collective-permute-start.7 = (bf16[192,896]{1,0:T(8,128)(2,1)S(1)}, bf16[192,896]{1,0:T(8,128)(2,1)}, u32[]{:S(2)}, u32[]{:S(2)}) collective-permute-start(bf16[192,896]{1,0:T(8,128)(2,1)S(1)} %get-tuple-element.14), channel_id=1, source_target_pairs={{0,16},{4,20},{16,0},{20,4},{8,24},{12,28},{24,8},{28,12},{1,17},{... | collective-permute-start | bytes 1032200 | tf_op jit(solution)/shard_map/ppermute | solution.py:68
  29.7 30.5 %copy-start.2 = (bf16[192,896]{1,0:T(8,128)(2,1)}, bf16[192,896]{1,0:T(8,128)(2,1)S(1)}, u32[]{:S(2)}) copy-start(bf16[192,896]{1,0:T(8,128)(2,1)S(1)} %collective-permute-done.2) | copy-start | bytes 1032196
  29.7 20.7 %collective-permute-start.4 = (bf16[192,896]{1,0:T(8,128)(2,1)S(1)}, bf16[192,896]{1,0:T(8,128)(2,1)S(1)}, u32[]{:S(2)}, u32[]{:S(2)}) collective-permute-start(bf16[192,896]{1,0:T(8,128)(2,1)S(1)} %collective-permute-done.2), channel_id=1, source_target_pairs={{8,0},{12,4},{16,24},{20,28},{9,1},{13,5},{17,25},{21,29},{10,2},{... | collective-permute-start | bytes 1032200 | tf_op jit(solution)/shard_map/ppermute | solution.py:70
  38.7 19.1 %all-to-all-start = ((bf16[4,192,512]{2,1,0:T(8,128)(2,1)}), bf16[4,192,512]{2,1,0:T(8,128)(2,1)S(1)}, u32[]{:S(2)}, u32[]{:S(2)}) async-start(bf16[4,192,512]{2,1,0:T(8,128)(2,1)} %stack.2), calls=%async_computation | async-start | bytes 1572864 | tf_op jit(solution)/shard_map/all_to_all | solution.py:47
  42.2 15.6 %collective-permute-start.1 = (bf16[192,896]{1,0:T(8,128)(2,1)S(1)}, bf16[192,896]{1,0:T(8,128)(2,1)}, u32[]{:S(2)}, u32[]{:S(2)}) collective-permute-start(bf16[192,896]{1,0:T(8,128)(2,1)S(1)} %get-tuple-element.13), channel_id=1, source_target_pairs={{0,8},{4,12},{8,0},{12,4},{16,24},{20,28},{24,16},{28,20},{1,9},{5... | collective-permute-start | bytes 1032200 | tf_op jit(solution)/shard_map/ppermute | solution.py:67
  42.5 19.2 %collective-permute-start.8 = (bf16[192,896]{1,0:T(8,128)(2,1)S(1)}, bf16[192,896]{1,0:T(8,128)(2,1)S(1)}, u32[]{:S(2)}, u32[]{:S(2)}) collective-permute-start(bf16[192,896]{1,0:T(8,128)(2,1)S(1)} %get-tuple-element.14), channel_id=1, source_target_pairs={{8,16},{12,20},{16,8},{20,12},{9,17},{13,21},{17,9},{21,13},{10,18... | collective-permute-start | bytes 1032200 | tf_op jit(solution)/shard_map/ppermute | solution.py:69
  43.2 29.0 %collective-permute-start.6 = (bf16[192,896]{1,0:T(8,128)(2,1)S(1)}, bf16[192,896]{1,0:T(8,128)(2,1)}, u32[]{:S(2)}, u32[]{:S(2)}) collective-permute-start(bf16[192,896]{1,0:T(8,128)(2,1)S(1)} %get-tuple-element.14), channel_id=1, source_target_pairs={{0,8},{4,12},{8,0},{12,4},{16,24},{20,28},{24,16},{28,20},{1,9},{5... | collective-permute-start | bytes 1032200 | tf_op jit(solution)/shard_map/ppermute | solution.py:67
  48.0 24.1 %collective-permute-start.9 = (bf16[192,896]{1,0:T(8,128)(2,1)}, bf16[192,896]{1,0:T(8,128)(2,1)S(1)}, u32[]{:S(2)}, u32[]{:S(2)}) collective-permute-start(bf16[192,896]{1,0:T(8,128)(2,1)} %collective-permute-done.7), channel_id=1, source_target_pairs={{8,0},{12,4},{16,24},{20,28},{9,1},{13,5},{17,25},{21,29},{10,2},{... | collective-permute-start | bytes 1032200 | tf_op jit(solution)/shard_map/ppermute | solution.py:70
  60.2 42.3 %collective-permute-start.5 = (bf16[256,896]{1,0:T(8,128)(2,1)}, bf16[256,896]{1,0:T(8,128)(2,1)}, u32[]{:S(2)}, u32[]{:S(2)}) collective-permute-start(bf16[256,896]{1,0:T(8,128)(2,1)} %convolution_convert_fusion.1), channel_id=1, source_target_pairs={{0,4},{4,0},{8,12},{12,8},{16,20},{20,16},{24,28},{28,24},{1,5},{5... | collective-permute-start | bytes 1376264 | tf_op jit(solution)/shard_map/ppermute | solution.py:75
  73.8 31.0 %collective-permute-start.10 = (bf16[256,896]{1,0:T(8,128)(2,1)S(1)}, bf16[256,896]{1,0:T(8,128)(2,1)S(1)}, u32[]{:S(2)}, u32[]{:S(2)}) collective-permute-start(bf16[256,896]{1,0:T(8,128)(2,1)S(1)} %convolution_convert_fusion), channel_id=1, source_target_pairs={{0,4},{4,0},{8,12},{12,8},{16,20},{20,16},{24,28},{28,24},{1,5},{5... | collective-permute-start | bytes 1376264 | tf_op jit(solution)/shard_map/ppermute | solution.py:75
